TPU v7x, 128 devices: a whole 4x4x4 slice. The times are simulated.
128 devices in a mesh: dp: 16 (over y, x_hi, core), fsdp: 8 (over z, x_lo).
Axes of the slice: x: 4 (x_hi: 2, x_lo: 2; x = x_hi * 2 + x_lo), y: 4, z: 4, core: 2. Of those that a mesh axis runs over, the one named last changes fastest.
Arguments:
- acts: bfloat16 [65536, 8192], P(('dp', 'fsdp')), may hold values from -24 to 24
- grad_out: bfloat16 [65536, 1024], P(('dp', 'fsdp')), may hold values from -24 to 24
- codes: int32 [128, 16, 1024], P('fsdp'), may hold values from 0 to 65535
- scale_codes: int32 [128, 1024], P('fsdp'), may hold values from 0 to 255
- col_scale: float32 [1024], replicated, may hold values from 0.03 to 0.3
- down_adapter: bfloat16 [64, 8192], P(None, 'fsdp'), may hold values from -0.1796875 to 0.1796875
- up_adapter: bfloat16 [64, 1024], P(None, 'fsdp'), may hold values from -0.1875 to 0.1875
Outputs:
- input_gradient: bfloat16 [65536, 8192], P(('dp', 'fsdp'))
- grad_down: float32 [64, 8192], P(None, 'fsdp')
- grad_up: float32 [64, 1024], P(None, 'fsdp')
All inputs are finite; a program needn't handle non-finite values.
Results may differ from a plain program's by a relative error of at most 0.0059.
Values may be sent and summed in bfloat16 or wider, within the bound.
No kernel may reach another device: no remote copies, remote signals or barrier semaphores. Data moves between devices by JAX's collectives and lax.ppermute only.
A program may use at most 128 MiB of HBM per device.

v0:
```python
import jax
import jax.numpy as jnp
from jax import lax
from jax.sharding import PartitionSpec as P

adapter_scale = 0.5
nf4_table = [
    -1.0,
    -0.6961928009986877,
    -0.5250730514526367,
    -0.39491748809814453,
    -0.28444138169288635,
    -0.18477343022823334,
    -0.09105003625154495,
    0.0,
    0.07958029955625534,
    0.16093020141124725,
    0.24611230194568634,
    0.33791524171829224,
    0.44070982933044434,
    0.5626170039176941,
    0.7229568362236023,
    1.0,
]


def joined_along(tiles, dim):
    tiles = jnp.moveaxis(tiles, 0, dim)
    lengths = tiles.shape
    return tiles.reshape(*lengths[:dim], lengths[dim] * lengths[dim + 1], *lengths[dim + 2 :])


def gather_packed(arrays, axis, dims):
    flat = jnp.concatenate([a.reshape(-1) for a in arrays])
    lines, at, gathered = (lax.all_gather(flat, axis), 0, [])
    for a, dim in zip(arrays, dims):
        tiles = lines[:, at : at + a.size].reshape(-1, *a.shape)
        gathered.append(joined_along(tiles, dim))
        at += a.size
    return tuple(gathered)


def in_blocks(value, dim, length):
    before, after = (value.shape[:dim], value.shape[dim + 1 :])
    return jnp.moveaxis(value.reshape(*before, length, -1, *after), dim, 0)


def sum_at_owner(value, axis, dim):
    tiles = in_blocks(value, dim, lax.axis_size(axis))
    arrived = lax.all_to_all(tiles, axis, split_axis=0, concat_axis=0, tiled=True)
    return arrived.astype(jnp.float32).sum(axis=0)


def copy_for_each(value, axis):
    length = lax.axis_size(axis)
    return lax.all_to_all(
        jnp.broadcast_to(value[None], (length, *value.shape)), axis, 0, 0, tiled=True
    )


def taken_together(value, axis):
    everything = copy_for_each(value, axis)
    return jnp.sum(everything.astype(jnp.float32), axis=0)


def dequantize(codes, scale_codes, col_scale):
    block_count = codes.shape[0]
    columns = codes.shape[2]
    nibbles = jnp.stack([codes >> 4 * nibble_pos & 15 for nibble_pos in range(4)], axis=2)
    levels = jnp.zeros(nibbles.shape, jnp.float32)
    for position, quantum in enumerate(nf4_table):
        levels = jnp.where(nibbles == position, jnp.float32(quantum), levels)
    absmax = (scale_codes.astype(jnp.float32) + 1.0) / 256.0 * col_scale[None, :]
    weight = levels * absmax[:, None, None, :]
    return weight.reshape(block_count * 64, columns).astype(jnp.bfloat16)


def local(acts, grad_out, codes, scale_codes, col_scale, down_adapter, up_adapter):
    down_full, up_full = gather_packed((down_adapter, up_adapter), "fsdp", (1, 1))
    mixed = jnp.dot(grad_out, up_full.T, preferred_element_type=jnp.float32).astype(jnp.bfloat16)
    lowered = jnp.dot(acts, down_full.T, preferred_element_type=jnp.float32).astype(jnp.bfloat16)
    token_count = acts.shape[0] * lax.axis_size("dp") * lax.axis_size("fsdp")
    scale_factor = adapter_scale * float(token_count) ** (-0.5)
    local_rows = dequantize(codes, scale_codes, col_scale)
    frozen_base = lax.dot_general(
        grad_out,
        lax.all_gather(local_rows, "fsdp", axis=0, tiled=True),
        (((1,), (1,)), ((), ())),
        preferred_element_type=jnp.float32,
    )
    operand_side = jnp.dot(mixed, down_full, preferred_element_type=jnp.float32)
    input_gradient = (frozen_base + adapter_scale * operand_side).astype(jnp.bfloat16)
    term_down = lax.dot_general(
        mixed, acts, (((0,), (0,)), ((), ())), preferred_element_type=jnp.float32
    )
    term_up = lax.dot_general(
        lowered, grad_out, (((0,), (0,)), ((), ())), preferred_element_type=jnp.float32
    )
    shard_down = sum_at_owner(term_down.astype(jnp.bfloat16), "fsdp", 1)
    shard_up = sum_at_owner(term_up.astype(jnp.bfloat16), "fsdp", 1)
    summed_down = taken_together(shard_down.astype(jnp.bfloat16), "dp").astype(jnp.float32)
    summed_up = taken_together(shard_up.astype(jnp.bfloat16), "dp").astype(jnp.float32)
    grad_down = scale_factor * summed_down
    grad_up = scale_factor * summed_up
    return (input_gradient, grad_down, grad_up)


def solution(mesh):
    placed = (
        P(("dp", "fsdp"), None),
        P(("dp", "fsdp"), None),
        P("fsdp", None, None),
        P("fsdp", None),
        P(),
        P(None, "fsdp"),
        P(None, "fsdp"),
    )
    return jax.shard_map(
        local,
        mesh=mesh,
        in_specs=placed,
        out_specs=(P(("dp", "fsdp"), None), P(None, "fsdp"), P(None, "fsdp")),
        check_vma=False,
    )
```

profile of v0, /device:TPU:1, one launch (start us, length us, event | category | flops | bytes accessed | tf_op | source)
XLA Modules:
  0.0 462.1 jit_solution(7870341430328449806)
XLA Ops:
  7.2 0.0 copy-start
  7.2 0.0 all-gather.6.cloned.1.call-start
  7.2 1.0 copy.31
  8.2 1.4 pad_maximum_fusion
  9.6 0.0 all-gather.6.cloned.1.call-update
  9.6 0.0 all-gather.4.cloned.1.call-start
  9.7 1.5 and_bitcast_fusion.3
  11.2 0.9 copy-done.2
  12.2 0.4 copy-done.3
  12.5 4.1 select_select_fusion
  16.6 4.8 %copy.23 = f32[16,16,4,1024]{3,2,1,0:T(4,128)} copy(f32[16,16,4,1024]{3,1,0,2:T(8,128)S(1)} %select_select_fusion) | data formatting | bytes 8388608 | tf_op jit(solution)/shard_map/jit(_where)/select_n | solution.py:72
  21.5 5.3 %reshape.108 = f32[1024,1024]{1,0:T(8,128)} reshape(f32[16,16,4,1024]{3,2,1,0:T(4,128)} %copy.23) | data formatting | bytes 8388608 | tf_op jit(solution)/shard_map/jit(_where)/select_n | solution.py:72
  26.8 2.2 fusion.1
  29.0 2.1 copy.22
  31.1 0.7 eq.156
  31.8 3.1 mul.45
  34.9 5.3 %mul.46 = f32[1024,1024]{1,0:T(8,128)} reshape(f32[16,16,4,1024]{3,2,1,0:T(4,128)} %mul.45) | data formatting | bytes 8388608 | tf_op jit(solution)/shard_map/mul | solution.py:74
  40.2 6.0 %multiply_convert_fusion = bf16[1024,1024]{1,0:T(8,128)(2,1)} fusion(f32[1024,1024]{1,0:T(8,128)} %mul.46, pred[1024,1024]{1,0:T(8,128)(4,1)S(1)} %eq.156, f32[1024,1024]{1,0:T(8,128)} %reshape.108), kind=kLoop, calls=%fused_computation.6 | loop fusion | flops 3145728 | bytes 11534336 | tf_op jit(solution)/shard_map/convert_element_type | solution.py:75
  46.3 0.0 all-gather.4.cloned.1.call-update
  46.3 2.7 all-gather.6.cloned.1.call-done
  49.0 1.8 reshape.92
  50.7 0.1 slice.9
  50.8 0.6 copy.33
  51.4 0.0 copy-done
  51.4 6.3 %fusion.2 = bf16[8,8,8,128]{3,2,1,0:T(8,128)(2,1)S(1)} fusion(bf16[512,1024]{1,0:T(8,128)(2,1)S(1)} %copy-done, bf16[64,8192]{1,0:T(8,128)(2,1)S(1)} %bitcast.52, bf16[512,8192]{1,0:T(8,128)(2,1)} %param.7), kind=kOutput, calls=%fused_computation.9 | convolution fusion | flops 604078080 | bytes 10616832 | tf_op jit(solution)/shard_map/dot_general | solution.py:96
  57.7 0.7 copy.41
  58.4 4.1 all-to-all-start.2
  62.5 0.4 convolution_convert_fusion.2
  63.0 5.6 %convolution_convert_fusion = bf16[64,8192]{1,0:T(8,128)(2,1)S(1)} fusion(bf16[64,512]{1,0:T(8,128)(2,1)S(1)} %convolution_convert_fusion.2, bf16[512,8192]{1,0:T(8,128)(2,1)} %param.7), kind=kOutput, calls=%fused_computation.2 | convolution fusion | flops 537395200 | bytes 9502720 | tf_op jit(solution)/shard_map/dot_general | solution.py:93
  68.6 1.1 copy.40
  69.7 0.0 all-to-all-done.2
  69.7 5.1 %all-to-all-start = ((bf16[8,64,1024]{2,1,0:T(8,128)(2,1)}), bf16[8,64,1024]{2,1,0:T(8,128)(2,1)S(1)}, u32[]{:S(2)}, u32[]{:S(2)}) async-start(bf16[8,64,1024]{2,1,0:T(8,128)(2,1)} %bitcast.54), calls=%async_computation | async-start | bytes 2097152 | tf_op jit(solution)/shard_map/all_to_all | solution.py:50
  74.8 25.6 %all-to-all-done = bf16[8,64,1024]{2,1,0:T(8,128)(2,1)S(1)} async-done(((bf16[8,64,1024]{2,1,0:T(8,128)(2,1)}), bf16[8,64,1024]{2,1,0:T(8,128)(2,1)S(1)}, u32[]{:S(2)}, u32[]{:S(2)}) %all-to-all-start) | async-done | bytes 1048608 | tf_op jit(solution)/shard_map/all_to_all | solution.py:50
  100.3 0.8 broadcast_in_dim.84
  101.1 12.4 %all-to-all-start.3 = ((bf16[16,64,128]{2,1,0:T(8,128)(2,1)}), bf16[16,64,128]{2,1,0:T(8,128)(2,1)S(1)}, u32[]{:S(2)}, u32[]{:S(2)}) async-start(bf16[16,64,128]{2,1,0:T(8,128)(2,1)} %broadcast_in_dim.84), calls=%async_computation.3 | async-start | bytes 524288 | tf_op jit(solution)/shard_map/all_to_all | solution.py:56
  113.5 0.8 reduce_sum.42
  114.4 11.2 %all-to-all-done.3 = bf16[16,64,128]{2,1,0:T(8,128)(2,1)S(1)} async-done(((bf16[16,64,128]{2,1,0:T(8,128)(2,1)}), bf16[16,64,128]{2,1,0:T(8,128)(2,1)S(1)}, u32[]{:S(2)}, u32[]{:S(2)}) %all-to-all-start.3) | async-done | bytes 262176 | tf_op jit(solution)/shard_map/all_to_all | solution.py:56
  125.5 2.5 broadcast_in_dim.83
  128.0 5.0 %all-to-all-start.1 = ((bf16[16,64,1024]{2,1,0:T(8,128)(2,1)}), bf16[16,64,1024]{2,1,0:T(8,128)(2,1)}, u32[]{:S(2)}, u32[]{:S(2)}) async-start(bf16[16,64,1024]{2,1,0:T(8,128)(2,1)} %broadcast_in_dim.83), calls=%async_computation.1 | async-start | bytes 4194304 | tf_op jit(solution)/shard_map/all_to_all | solution.py:56
  133.1 0.6 broadcast_multiply_fusion.1
  133.7 50.9 %all-to-all-done.1 = bf16[16,64,1024]{2,1,0:T(8,128)(2,1)} async-done(((bf16[16,64,1024]{2,1,0:T(8,128)(2,1)}), bf16[16,64,1024]{2,1,0:T(8,128)(2,1)}, u32[]{:S(2)}, u32[]{:S(2)}) %all-to-all-start.1) | async-done | bytes 2097184 | tf_op jit(solution)/shard_map/all_to_all | solution.py:56
  184.6 2.0 convert_reduce_fusion
  186.6 0.7 broadcast_multiply_fusion
  187.3 230.9 %all-gather.4.cloned.1.call-done = bf16[8192,1024]{1,0:T(8,128)(2,1)} async-done(((bf16[1024,1024]{1,0:T(8,128)(2,1)}), bf16[8192,1024]{1,0:T(8,128)(2,1)}) %all-gather.4.cloned.1.call-update) | async-done | bytes 16777232 | tf_op jit(solution)/shard_map/all_gather | solution.py:87
  418.3 15.8 %fusion.5 = f32[8192,512]{1,0:T(8,128)} fusion(bf16[8192,1024]{1,0:T(8,128)(2,1)} %all-gather.4.cloned.1.call-done, bf16[512,1024]{1,0:T(8,128)(2,1)S(1)} %copy-done), kind=kOutput, calls=%fused_computation.26 | convolution fusion | flops 8589934592 | bytes 34603008 | tf_op jit(solution)/shard_map/dot_general | solution.py:85
  434.0 9.2 %fusion = bf16[512,8192]{0,1:T(8,128)(2,1)} fusion(f32[8192,512]{1,0:T(8,128)} %fusion.5, bf16[64,512]{1,0:T(8,128)(2,1)S(1)} %convolution_convert_fusion.2, bf16[64,8192]{1,0:T(8,128)(2,1)S(1)} %bitcast.53), kind=kOutput, calls=%fused_computation.1 | convolution fusion | flops 549453824 | bytes 26279936 | tf_op jit(solution)/shard_map/dot_general | solution.py:91
  443.3 12.0 %copy.27 = bf16[512,8192]{1,0:T(8,128)(2,1)} copy(bf16[512,8192]{0,1:T(8,128)(2,1)} %fusion) | data formatting | bytes 16777216
  455.3 0.0 copy-done.1
  (12 shorter events, 0.1 us)
Async XLA Ops:
  7.2 44.3 %copy-start = (bf16[512,1024]{1,0:T(8,128)(2,1)S(1)}, bf16[512,1024]{1,0:T(8,128)(2,1)}, u32[]{:S(2)}) copy-start(bf16[512,1024]{1,0:T(8,128)(2,1)} %param.8) | copy-start | bytes 3145732
  7.2 41.8 %all-gather.6.cloned.1.call-start = ((), (), s32[]{:S(2)}) async-start(), calls=%async_computation.5 | async-start | bytes 1327104 | tf_op jit(solution)/shard_map/all_gather | solution.py:35
  9.6 408.6 %all-gather.4.cloned.1.call-start = ((), (), s32[]{:S(2)}) async-start(), calls=%async_computation.4 | async-start | bytes 18874368 | tf_op jit(solution)/shard_map/all_gather | solution.py:87
  11.2 1.0 copy-start.2
  11.2 1.3 copy-start.3
  26.8 5.0 %copy-start.5 = (f32[1024]{0:T(1024)S(1)}, f32[1024]{0:T(1024)}, u32[]{:S(2)}) copy-start(f32[1024]{0:T(1024)} %param.11) | copy-start | bytes 12292
  26.8 5.0 %copy-start.4 = (s32[16,1024]{1,0:T(8,128)S(1)}, s32[16,1024]{1,0:T(8,128)}, u32[]{:S(2)}) copy-start(s32[16,1024]{1,0:T(8,128)} %param.10) | copy-start | bytes 196612
  58.4 11.2 %all-to-all-start.2 = ((bf16[8,64,128]{2,1,0:T(8,128)(2,1)}), bf16[8,64,128]{2,1,0:T(8,128)(2,1)S(1)}, u32[]{:S(2)}, u32[]{:S(2)}) async-start(bf16[8,64,128]{2,1,0:T(8,128)(2,1)} %bitcast.51), calls=%async_computation.2 | async-start | bytes 262144 | tf_op jit(solution)/shard_map/all_to_all | solution.py:50
  69.7 30.7 %all-to-all-start = ((bf16[8,64,1024]{2,1,0:T(8,128)(2,1)}), bf16[8,64,1024]{2,1,0:T(8,128)(2,1)S(1)}, u32[]{:S(2)}, u32[]{:S(2)}) async-start(bf16[8,64,1024]{2,1,0:T(8,128)(2,1)} %bitcast.54), calls=%async_computation | async-start | bytes 2097152 | tf_op jit(solution)/shard_map/all_to_all | solution.py:50
  101.1 24.4 %all-to-all-start.3 = ((bf16[16,64,128]{2,1,0:T(8,128)(2,1)}), bf16[16,64,128]{2,1,0:T(8,128)(2,1)S(1)}, u32[]{:S(2)}, u32[]{:S(2)}) async-start(bf16[16,64,128]{2,1,0:T(8,128)(2,1)} %broadcast_in_dim.84), calls=%async_computation.3 | async-start | bytes 524288 | tf_op jit(solution)/shard_map/all_to_all | solution.py:56
  128.0 56.5 %all-to-all-start.1 = ((bf16[16,64,1024]{2,1,0:T(8,128)(2,1)}), bf16[16,64,1024]{2,1,0:T(8,128)(2,1)}, u32[]{:S(2)}, u32[]{:S(2)}) async-start(bf16[16,64,1024]{2,1,0:T(8,128)(2,1)} %broadcast_in_dim.83), calls=%async_computation.1 | async-start | bytes 4194304 | tf_op jit(solution)/shard_map/all_to_all | solution.py:56
  443.3 12.0 %copy-start.1 = (bf16[512,1024]{1,0:T(8,128)(2,1)S(1)}, bf16[512,1024]{1,0:T(8,128)(2,1)}, u32[]{:S(2)}) copy-start(bf16[512,1024]{1,0:T(8,128)(2,1)} %param.8) | copy-start | bytes 3145732
Sparse Core Ops, SparseCore 0:
  10.2 38.7 all-gather.5
  51.2 367.0 all-gather.3
where the time goes:
time: 463 us; the launch traced here: 462 us
  waiting for transfers between devices  321 us (69%)
  local copies, waits for them, and re-layouts  43.1 us (9%)
  matrix products  37.4 us (8%)
  starting transfers between devices  26.7 us (6%)
  other arithmetic  19.5 us (4%)
  between operations  14.2 us (3%)
    all_gather x1, waiting for transfers between devices, local(): lax.all_gather(local_rows, 'fsdp', axis=0, tiled=True)  231 us
    all_to_all x2, waiting for transfers between devices, copy_for_each(): lax.all_to_all(jnp.broadcast_to(value[None], (length, *value.shape)), axi...  62 us
    all_to_all x2, waiting for transfers between devices, sum_at_owner(): lax.all_to_all(tiles, axis, split_axis=0, concat_axis=0, tiled=True)  25.6 us
    all_to_all x2, starting transfers between devices, copy_for_each(): lax.all_to_all(jnp.broadcast_to(value[None], (length, *value.shape)), axi...  17.4 us
    dot_general x1, matrix products, local(): lax.dot_general(grad_out, lax.all_gather(local_rows, 'fsdp', axis=0, tile...  15.8 us
    unnamed x15, local copies, waits for them, and re-layouts  14.9 us
    select_n x2, local copies, waits for them, and re-layouts, dequantize(): levels = jnp.where(nibbles == position, jnp.float32(quantum), levels)  10.2 us
  transfers between devices with their start and end apart: 6, of which 5 were waited for; matrix products, arithmetic and copies ran while one was open for 13% of the time, Pallas kernels for 0%

commit v1 on v0

--- a/solution.py
+++ b/solution.py
@@ -84,7 +84,9 @@
     local_rows = dequantize(codes, scale_codes, col_scale)
     frozen_base = lax.dot_general(
         grad_out,
-        lax.all_gather(local_rows, "fsdp", axis=0, tiled=True),
+        jnp.concatenate(
+            lax.all_to_all(jnp.stack([local_rows] * lax.axis_size("fsdp")), "fsdp", 0, 0), axis=0
+        ),
         (((1,), (1,)), ((), ())),
         preferred_element_type=jnp.float32,
     )

time: 463 us -> 391 us (0.84)
  waiting for transfers between devices: 321 us -> 233 us
  starting transfers between devices: 26.7 us -> 33.4 us
  local copies, waits for them, and re-layouts: 43.1 us -> 49.2 us
    all_gather x1 -> x0, waiting for transfers between devices: 231 us -> none  [local(): lax.all_gather(local_rows, 'fsdp', axis=0, tiled=True)]
    all_to_all x0 -> x1, waiting for transfers between devices: none -> 180 us  [local(): lax.all_to_all(jnp.stack([local_rows] * lax.axis_size('fsdp')), 'fsdp', 0...]
    all_to_all x2, waiting for transfers between devices: 62 us -> 3.51 us  [copy_for_each(): lax.all_to_all(jnp.broadcast_to(value[None], (length, *value.shape)), axi...]
    all_gather x1, waiting for transfers between devices: 2.66 us -> 39.3 us  [gather_packed(): lines, at, gathered = (lax.all_gather(flat, axis), 0, [])]
    all_to_all x2, waiting for transfers between devices: 25.6 us -> 10.4 us  [sum_at_owner(): lax.all_to_all(tiles, axis, split_axis=0, concat_axis=0, tiled=True)]
    another operation x0 -> x1, local copies, waits for them, and re-layouts: none -> 6.02 us  [local(): jnp.stack([local_rows] * lax.axis_size('fsdp'))]
    all_to_all x0 -> x1, starting transfers between devices: none -> 5.97 us  [local(): lax.all_to_all(jnp.stack([local_rows] * lax.axis_size('fsdp')), 'fsdp', 0...]
  transfers between devices with their start and end apart: 6 -> 6, of which waited for: 5 -> 4; matrix products, arithmetic and copies ran while one was open for 13% -> 13% of each run, Pallas kernels for 0% -> 0%
where the time goes in v1:
time: 391 us; the launch traced here: 389 us
  waiting for transfers between devices  233 us (60%)
  local copies, waits for them, and re-layouts  49.2 us (13%)
  matrix products  36.7 us (9%)
  starting transfers between devices  33.4 us (9%)
  other arithmetic  22.4 us (6%)
  between operations  14.2 us (4%)
    all_to_all x1, waiting for transfers between devices, local(): lax.all_to_all(jnp.stack([local_rows] * lax.axis_size('fsdp')), 'fsdp', 0...  180 us
    all_gather x1, waiting for transfers between devices, gather_packed(): lines, at, gathered = (lax.all_gather(flat, axis), 0, [])  39.3 us
    all_to_all x2, starting transfers between devices, copy_for_each(): lax.all_to_all(jnp.broadcast_to(value[None], (length, *value.shape)), axi...  19 us
    dot_general x1, matrix products, local(): lax.dot_general(grad_out, jnp.concatenate(lax.all_to_all(jnp.stack([local...  15.8 us
    unnamed x15, local copies, waits for them, and re-layouts  13.8 us
    all_to_all x2, waiting for transfers between devices, sum_at_owner(): lax.all_to_all(tiles, axis, split_axis=0, concat_axis=0, tiled=True)  10.4 us
    select_n x2, local copies, waits for them, and re-layouts, dequantize(): levels = jnp.where(nibbles == position, jnp.float32(quantum), levels)  10.1 us
    dot_general x1, matrix products, local(): operand_side = jnp.dot(mixed, down_full, preferred_element_type=jnp.float32)  9.21 us
  transfers between devices with their start and end apart: 6, of which 4 were waited for; matrix products, arithmetic and copies ran while one was open for 13% of the time, Pallas kernels for 0%

profile of v1, /device:TPU:1, one launch (start us, length us, event | category | flops | bytes accessed | tf_op | source)
XLA Modules:
  0.0 389.4 jit_solution(3053156096834672124)
XLA Ops:
  7.2 0.0 copy-start
  7.2 0.0 all-gather.3.cloned.1.call-start
  7.2 1.0 copy.31
  8.2 1.4 pad_maximum_fusion
  9.6 0.0 all-gather.3.cloned.1.call-update
  9.6 39.3 %all-gather.3.cloned.1.call-done = bf16[589824]{0:T(1024)(128)(2,1)} async-done(((bf16[73728]{0:T(1024)(128)(2,1)}), bf16[589824]{0:T(1024)(128)(2,1)}) %all-gather.3.cloned.1.call-update) | async-done | bytes 1179664 | tf_op jit(solution)/shard_map/all_gather | solution.py:35
  49.0 1.8 reshape.101
  50.7 0.1 slice.9
  50.8 0.6 copy.33
  51.4 0.0 copy-start.1
  51.4 0.0 copy-done
  51.4 0.4 convolution_convert_fusion.2
  51.9 6.3 %fusion.2 = bf16[8,8,8,128]{3,2,1,0:T(8,128)(2,1)S(1)} fusion(bf16[512,1024]{1,0:T(8,128)(2,1)S(1)} %copy-done, bf16[64,8192]{1,0:T(8,128)(2,1)S(1)} %bitcast.53, bf16[512,8192]{1,0:T(8,128)(2,1)} %param.7), kind=kOutput, calls=%fused_computation.9 | convolution fusion | flops 604078080 | bytes 10616832 | tf_op jit(solution)/shard_map/dot_general | solution.py:98
  58.2 0.0 copy-done.1
  58.2 0.7 copy.41
  58.9 3.4 all-to-all-start.3
  62.3 5.0 %convolution_convert_fusion = bf16[64,8192]{1,0:T(8,128)(2,1)S(1)} fusion(bf16[64,512]{1,0:T(8,128)(2,1)S(1)} %convolution_convert_fusion.2, bf16[512,8192]{1,0:T(8,128)(2,1)} %param.7), kind=kOutput, calls=%fused_computation.2 | convolution fusion | flops 537395200 | bytes 9502720 | tf_op jit(solution)/shard_map/dot_general | solution.py:95
  67.2 1.1 copy.40
  68.3 0.0 all-to-all-done.3
  68.3 5.1 %all-to-all-start.1 = ((bf16[8,64,1024]{2,1,0:T(8,128)(2,1)}), bf16[8,64,1024]{2,1,0:T(8,128)(2,1)S(1)}, u32[]{:S(2)}, u32[]{:S(2)}) async-start(bf16[8,64,1024]{2,1,0:T(8,128)(2,1)} %bitcast.50), calls=%async_computation.1 | async-start | bytes 2097152 | tf_op jit(solution)/shard_map/all_to_all | solution.py:50
  73.4 10.4 %all-to-all-done.1 = bf16[8,64,1024]{2,1,0:T(8,128)(2,1)S(1)} async-done(((bf16[8,64,1024]{2,1,0:T(8,128)(2,1)}), bf16[8,64,1024]{2,1,0:T(8,128)(2,1)S(1)}, u32[]{:S(2)}, u32[]{:S(2)}) %all-to-all-start.1) | async-done | bytes 1048608 | tf_op jit(solution)/shard_map/all_to_all | solution.py:50
  83.7 0.8 broadcast_in_dim.84
  84.6 0.2 copy-done.3
  84.8 13.9 %all-to-all-start.4 = ((bf16[16,64,128]{2,1,0:T(8,128)(2,1)}), bf16[16,64,128]{2,1,0:T(8,128)(2,1)S(1)}, u32[]{:S(2)}, u32[]{:S(2)}) async-start(bf16[16,64,128]{2,1,0:T(8,128)(2,1)} %broadcast_in_dim.84), calls=%async_computation.4 | async-start | bytes 524288 | tf_op jit(solution)/shard_map/all_to_all | solution.py:56
  98.7 3.1 and_bitcast_fusion.3
  101.8 2.1 reduce_sum.42
  103.9 3.5 all-to-all-done.4
  107.4 2.5 broadcast_in_dim.83
  109.9 5.1 %all-to-all-start.2 = ((bf16[16,64,1024]{2,1,0:T(8,128)(2,1)}), bf16[16,64,1024]{2,1,0:T(8,128)(2,1)}, u32[]{:S(2)}, u32[]{:S(2)}) async-start(bf16[16,64,1024]{2,1,0:T(8,128)(2,1)} %broadcast_in_dim.83), calls=%async_computation.2 | async-start | bytes 4194304 | tf_op jit(solution)/shard_map/all_to_all | solution.py:56
  115.0 5.2 %select_select_fusion = f32[16,16,4,1024]{3,1,0,2:T(8,128)S(1)} fusion(s32[16,16,1,1024]{3,1,0,2:T(8,128)} %get-tuple-element.17, s32[16,16,1,1024]{3,1,0,2:T(8,128)} %get-tuple-element.18, s32[16,16,1,1024]{3,1,0,2:T(8,128)S(1)} %get-tuple-element.16, s32[16,16,1,1024]{3,1,0,2:T(8,128)S(1)} %get-tuple-element.15), kind=kLoop, calls=%fused_computation.4 | loop fusion | flops 34603008 | bytes 8388608 | tf_op jit(solution)/shard_map/jit(_where)/select_n | solution.py:72
  120.2 4.8 %copy.23 = f32[16,16,4,1024]{3,2,1,0:T(4,128)} copy(f32[16,16,4,1024]{3,1,0,2:T(8,128)S(1)} %select_select_fusion) | data formatting | bytes 8388608 | tf_op jit(solution)/shard_map/jit(_where)/select_n | solution.py:72
  125.0 5.3 %reshape.117 = f32[1024,1024]{1,0:T(8,128)} reshape(f32[16,16,4,1024]{3,2,1,0:T(4,128)} %copy.23) | data formatting | bytes 8388608 | tf_op jit(solution)/shard_map/jit(_where)/select_n | solution.py:72
  130.3 2.2 fusion.1
  132.5 2.1 copy.22
  134.6 1.9 eq.188
  136.5 3.1 mul.47
  139.6 5.3 %mul.48 = f32[1024,1024]{1,0:T(8,128)} reshape(f32[16,16,4,1024]{3,2,1,0:T(4,128)} %mul.47) | data formatting | bytes 8388608 | tf_op jit(solution)/shard_map/mul | solution.py:74
  144.9 5.0 %multiply_convert_fusion = bf16[1024,1024]{1,0:T(8,128)(2,1)S(1)} fusion(f32[1024,1024]{1,0:T(8,128)} %mul.48, pred[1024,1024]{1,0:T(8,128)(4,1)} %eq.188, f32[1024,1024]{1,0:T(8,128)} %reshape.117), kind=kLoop, calls=%fused_computation.6 | loop fusion | flops 3145728 | bytes 11534336 | tf_op jit(solution)/shard_map/convert_element_type | solution.py:75
  149.9 0.0 all-to-all-done.2
  149.9 6.0 %stack.31 = bf16[8,1024,1024]{2,1,0:T(8,128)(2,1)} broadcast(bf16[1024,1024]{1,0:T(8,128)(2,1)S(1)} %multiply_convert_fusion), dimensions={1,2} | broadcast | bytes 18874368 | tf_op jit(solution)/shard_map/stack | solution.py:88
  155.9 6.0 %all-to-all-start = ((bf16[8,1024,1024]{2,1,0:T(8,128)(2,1)}), bf16[8,1024,1024]{2,1,0:T(8,128)(2,1)}, u32[]{:S(2)}, u32[]{:S(2)}) async-start(bf16[8,1024,1024]{2,1,0:T(8,128)(2,1)} %stack.31), calls=%async_computation | async-start | bytes 33554432 | tf_op jit(solution)/shard_map/all_to_all | solution.py:88
  162.0 0.6 broadcast_multiply_fusion.1
  162.6 2.0 convert_reduce_fusion
  164.6 0.7 broadcast_multiply_fusion
  165.3 180.3 %all-to-all-done = bf16[8,1024,1024]{2,1,0:T(8,128)(2,1)} async-done(((bf16[8,1024,1024]{2,1,0:T(8,128)(2,1)}), bf16[8,1024,1024]{2,1,0:T(8,128)(2,1)}, u32[]{:S(2)}, u32[]{:S(2)}) %all-to-all-start) | async-done | bytes 16777248 | tf_op jit(solution)/shard_map/all_to_all | solution.py:88
  345.6 15.8 %fusion.5 = f32[8192,512]{1,0:T(8,128)} fusion(bf16[8192,1024]{1,0:T(8,128)(2,1)} %bitcast.4, bf16[512,1024]{1,0:T(8,128)(2,1)S(1)} %copy-done), kind=kOutput, calls=%fused_computation.26 | convolution fusion | flops 8589934592 | bytes 34603008 | tf_op jit(solution)/shard_map/dot_general | solution.py:85
  361.5 9.2 %fusion = bf16[512,8192]{0,1:T(8,128)(2,1)} fusion(f32[8192,512]{1,0:T(8,128)} %fusion.5, bf16[64,512]{1,0:T(8,128)(2,1)S(1)} %convolution_convert_fusion.2, bf16[64,8192]{1,0:T(8,128)(2,1)S(1)} %bitcast.54), kind=kOutput, calls=%fused_computation.1 | convolution fusion | flops 549453824 | bytes 26279936 | tf_op jit(solution)/shard_map/dot_general | solution.py:93
  370.7 11.9 %copy.27 = bf16[512,8192]{1,0:T(8,128)(2,1)} copy(bf16[512,8192]{0,1:T(8,128)(2,1)} %fusion) | data formatting | bytes 16777216
  (12 shorter events, 0.1 us)
Async XLA Ops:
  7.2 44.3 %copy-start = (bf16[512,1024]{1,0:T(8,128)(2,1)S(1)}, bf16[512,1024]{1,0:T(8,128)(2,1)}, u32[]{:S(2)}) copy-start(bf16[512,1024]{1,0:T(8,128)(2,1)} %param.8) | copy-start | bytes 3145732
  7.2 41.8 %all-gather.3.cloned.1.call-start = ((), (), s32[]{:S(2)}) async-start(), calls=%async_computation.5 | async-start | bytes 1327104 | tf_op jit(solution)/shard_map/all_gather | solution.py:35
  51.4 6.8 %copy-start.1 = (bf16[8,8,8,1024]{3,1,2,0:T(8,128)(2,1)}, bf16[8,8,8,1024]{3,1,2,0:T(8,128)(2,1)S(1)}, u32[]{:S(2)}) copy-start(bf16[8,8,8,1024]{3,1,2,0:T(8,128)(2,1)S(1)} %copy.33) | copy-start | bytes 3145732
  58.9 9.4 %all-to-all-start.3 = ((bf16[8,64,128]{2,1,0:T(8,128)(2,1)}), bf16[8,64,128]{2,1,0:T(8,128)(2,1)S(1)}, u32[]{:S(2)}, u32[]{:S(2)}) async-start(bf16[8,64,128]{2,1,0:T(8,128)(2,1)} %bitcast.52), calls=%async_computation.3 | async-start | bytes 262144 | tf_op jit(solution)/shard_map/all_to_all | solution.py:50
  68.3 15.5 %all-to-all-start.1 = ((bf16[8,64,1024]{2,1,0:T(8,128)(2,1)}), bf16[8,64,1024]{2,1,0:T(8,128)(2,1)S(1)}, u32[]{:S(2)}, u32[]{:S(2)}) async-start(bf16[8,64,1024]{2,1,0:T(8,128)(2,1)} %bitcast.50), calls=%async_computation.1 | async-start | bytes 2097152 | tf_op jit(solution)/shard_map/all_to_all | solution.py:50
  83.7 1.1 copy-start.3
  84.8 22.6 %all-to-all-start.4 = ((bf16[16,64,128]{2,1,0:T(8,128)(2,1)}), bf16[16,64,128]{2,1,0:T(8,128)(2,1)S(1)}, u32[]{:S(2)}, u32[]{:S(2)}) async-start(bf16[16,64,128]{2,1,0:T(8,128)(2,1)} %broadcast_in_dim.84), calls=%async_computation.4 | async-start | bytes 524288 | tf_op jit(solution)/shard_map/all_to_all | solution.py:56
  109.9 40.0 %all-to-all-start.2 = ((bf16[16,64,1024]{2,1,0:T(8,128)(2,1)}), bf16[16,64,1024]{2,1,0:T(8,128)(2,1)}, u32[]{:S(2)}, u32[]{:S(2)}) async-start(bf16[16,64,1024]{2,1,0:T(8,128)(2,1)} %broadcast_in_dim.83), calls=%async_computation.2 | async-start | bytes 4194304 | tf_op jit(solution)/shard_map/all_to_all | solution.py:56
  130.3 6.2 %copy-start.5 = (f32[1024]{0:T(1024)S(1)}, f32[1024]{0:T(1024)}, u32[]{:S(2)}) copy-start(f32[1024]{0:T(1024)} %param.11) | copy-start | bytes 12292
  130.3 6.2 %copy-start.4 = (s32[16,1024]{1,0:T(8,128)S(1)}, s32[16,1024]{1,0:T(8,128)}, u32[]{:S(2)}) copy-start(s32[16,1024]{1,0:T(8,128)} %param.10) | copy-start | bytes 196612
  155.9 189.7 %all-to-all-start = ((bf16[8,1024,1024]{2,1,0:T(8,128)(2,1)}), bf16[8,1024,1024]{2,1,0:T(8,128)(2,1)}, u32[]{:S(2)}, u32[]{:S(2)}) async-start(bf16[8,1024,1024]{2,1,0:T(8,128)(2,1)} %stack.31), calls=%async_computation | async-start | bytes 33554432 | tf_op jit(solution)/shard_map/all_to_all | solution.py:88
  345.6 15.9 %copy-start.2 = (bf16[8,8,8,1024]{3,1,2,0:T(8,128)(2,1)S(1)}, bf16[8,8,8,1024]{3,1,2,0:T(8,128)(2,1)}, u32[]{:S(2)}) copy-start(bf16[8,8,8,1024]{3,1,2,0:T(8,128)(2,1)} %copy-done.1) | copy-start | bytes 3145732
Sparse Core Ops, SparseCore 0:
  10.2 38.7 all-gather.2
